TPU v7x, 512 devices: a whole 4x8x8 slice. The times are simulated.
512 devices in a mesh: lon: 64 (over z_lo, y, core), lat: 8 (over x, z_hi).
Axes of the slice: x: 4, y: 8, z: 8 (z_hi: 2, z_lo: 4; z = z_hi * 4 + z_lo), core: 2. Of those that a mesh axis runs over, the one named last changes fastest.
Arguments:
- prediction: bfloat16 [384, 1536, 222], P('lat', 'lon'), may hold values from -40 to 40
- observed_state: bfloat16 [384, 1536, 222], P('lat', 'lon'), may hold values from -40 to 40
- mean_state: bfloat16 [384, 1536, 222], P('lat', 'lon'), may hold values from -6 to 6
- usable_point_flags: int32 [384, 1536], P('lat', 'lon'), may hold values 0 or 1
- eastward_offsets: int32 [8], replicated, may hold values from 0 to 335, as said below
Outputs:
- correlation: float32 [8, 1536, 222], P('lat', 'lon')
Inputs may be any that keep to these rules, and one draw needn't show every extreme that they name: `eastward_offsets`: every lag lies below 336, and some lag equals 335.
All inputs are finite; a program needn't handle non-finite values. No bound on the sum of `usable_point_flags` on one device may be relied on, other than what follows from the above.
Results may differ from a plain program's by a relative error of at most 0.0044.
Values may be sent and summed in bfloat16 or wider, within the bound.
No kernel may reach another device: no remote copies, remote signals or barrier semaphores. Data moves between devices by JAX's collectives and lax.ppermute only.
A program may use at most 64 MiB of HBM per device.

v0:
```python
import jax
import jax.numpy as jnp
from jax import lax
from jax.sharding import PartitionSpec as P

REACH = 14


regular_term = 0.001


def from_behind(value, axis, by):
    count = lax.axis_size(axis)
    return lax.ppermute(value, axis, [(i, (i + by) % count) for i in range(count)])


def in_blocks(value, dim, count):
    before, after = (value.shape[:dim], value.shape[dim + 1 :])
    return jnp.moveaxis(value.reshape(*before, count, -1, *after), dim, 0)


def sent_and_summed(value, axis, dim):
    count = lax.axis_size(axis)
    blocks = lax.all_to_all(in_blocks(value, dim, count), axis, 0, 0, tiled=True)
    return jnp.sum(blocks.astype(jnp.float32), axis=0)


def in_one_piece(arrays, axis, dim, along):
    both = jnp.concatenate(arrays, axis=along)
    filled, at, gathered = (sent_and_summed(both, axis, dim), 0, [])
    for a in arrays:
        gathered.append(lax.slice_in_dim(filled, at, at + a.shape[along], axis=along))
        at += a.shape[along]
    return tuple(gathered)


def local(prediction, observed_state, mean_state, usable_point_flags, eastward_offsets):
    meridian_extent, parallel_extent, field_total = prediction.shape
    total_rows = meridian_extent * lax.axis_size("lat")
    row_index = (
        lax.axis_index("lat") * meridian_extent + jnp.arange(meridian_extent, dtype=jnp.int32)
    ).astype(jnp.float32)
    weights = jnp.cos(jnp.pi * ((row_index + 0.5) / total_rows - 0.5))
    predicted_mean_state = mean_state.astype(jnp.float32)
    prediction_departure = prediction.astype(jnp.float32) - predicted_mean_state
    observed_departure = (observed_state.astype(jnp.float32) - predicted_mean_state).astype(
        jnp.bfloat16
    )
    base_weight = weights[:, None] * usable_point_flags.astype(jnp.float32)
    window_cols = (REACH + 1) * parallel_extent
    start_true = jnp.zeros((meridian_extent, window_cols, field_total), jnp.bfloat16)
    start_true = lax.dynamic_update_slice_in_dim(start_true, observed_departure, 0, 1)
    start_valid = jnp.zeros((meridian_extent, window_cols), jnp.int32)
    start_valid = lax.dynamic_update_slice_in_dim(start_valid, usable_point_flags, 0, 1)

    def advance(turn_index, state_tuple):
        buffer_true, buffer_valid, slab_true, slab_valid = state_tuple
        slab_true, slab_valid = from_behind((slab_true, slab_valid), "lon", -1)
        place = (turn_index + 1) * parallel_extent
        buffer_true = lax.dynamic_update_slice_in_dim(buffer_true, slab_true, place, 1)
        buffer_valid = lax.dynamic_update_slice_in_dim(buffer_valid, slab_valid, place, 1)
        return (buffer_true, buffer_valid, slab_true, slab_valid)

    win_true, win_valid, unused_true, unused_valid = lax.fori_loop(
        0, REACH, advance, (start_true, start_valid, observed_departure, usable_point_flags)
    )

    def lag_sums(offset):
        frame_segment = lax.dynamic_slice_in_dim(win_true, offset, parallel_extent, 1).astype(
            jnp.float32
        )
        piece_valid = lax.dynamic_slice_in_dim(win_valid, offset, parallel_extent, 1).astype(
            jnp.float32
        )
        couple_factor = (base_weight * piece_valid)[:, :, None]
        joint_moment = jnp.sum(couple_factor * prediction_departure * frame_segment, axis=0)
        prediction_spread = jnp.sum(
            couple_factor * prediction_departure * prediction_departure, axis=0
        )
        var_true = jnp.sum(couple_factor * frame_segment * frame_segment, axis=0)
        return (joint_moment, prediction_spread, var_true)

    joint_moment, prediction_spread, var_true = lax.map(lag_sums, eastward_offsets)
    joint_moment, prediction_spread, var_true = in_one_piece(
        (
            joint_moment.astype(jnp.bfloat16),
            prediction_spread.astype(jnp.bfloat16),
            var_true.astype(jnp.bfloat16),
        ),
        "lat",
        0,
        1,
    )
    return joint_moment / jnp.sqrt((prediction_spread + regular_term) * (var_true + regular_term))


def solution(mesh):
    placed = (
        P("lat", "lon", None),
        P("lat", "lon", None),
        P("lat", "lon", None),
        P("lat", "lon"),
        P(),
    )
    return jax.shard_map(
        local, mesh=mesh, in_specs=placed, out_specs=P("lat", "lon", None), check_vma=False
    )
```

profile of v0, /device:TPU:1, one launch (start us, length us, event | category | flops | bytes accessed | tf_op | source)
XLA Modules:
  0.0 297.5 jit_solution(7430334140599943639)
XLA Ops:
  2.6 4.0 %dynamic_update_slice.30 = bf16[48,360,222]{2,1,0:T(8,128)(2,1)} pad(bf16[48,24,222]{2,1,0:T(8,128)(2,1)S(1)} %get-tuple-element.298, bf16[]{:T(256)} %constant.59.clone.1), padding=0_0x0_336x0_0 | pad | bytes 8183810 | tf_op jit(solution)/shard_map/dynamic_update_slice | solution.py:52
  6.6 234.8 %while.33 = (s32[]{:T(128)}, bf16[48,360,222]{2,1,0:T(8,128)(2,1)}, s32[48,360]{1,0:T(8,128)S(1)}, bf16[48,24,222]{2,1,0:T(8,128)(2,1)S(1)}, s32[48,24]{1,0:T(8,...) while((s32[]{:T(128)}, bf16[48,360,222]{2,1,0:T(8,128)(2,1)}, s32[48,360]{1,0:T(8,128)S(1)}, ...), condition=%wide.region_1.0_spmd, body=%wide.region_0.0_spmd.sunk | while | flops 6 | bytes 4207331 | solution.py:64
  6.6 8.9 %collective-permute-start = (bf16[48,24,222]{2,1,0:T(8,128)(2,1)S(1)}, bf16[48,24,222]{2,1,0:T(8,128)(2,1)S(1)}, u32[]{:S(2)}, u32[]{:S(2)}) collective-permute-start(bf16[48,24,222]{2,1,0:T(8,128)(2,1)S(1)} %get-tuple-element.307), channel_id=1, source_target_pairs={{0,504},{8,0},{16,8},{24,16},{32,24},{40,32},{48,40},{56,48},{64,5... | collective-permute-start | bytes 1534472 | tf_op jit(solution)/shard_map/while/body/eval_jaxpr/ppermute | solution.py:14
  15.5 4.9 %collective-permute-start.1 = (s32[48,24]{1,0:T(8,128)S(1)}, s32[48,24]{1,0:T(8,128)S(1)}, u32[]{:S(2)}, u32[]{:S(2)}) collective-permute-start(s32[48,24]{1,0:T(8,128)S(1)} %get-tuple-element.308), channel_id=1, source_target_pairs={{0,504},{8,0},{16,8},{24,16},{32,24},{40,32},{48,40},{56,48},{64,5... | collective-permute-start | bytes 13832 | tf_op jit(solution)/shard_map/while/body/eval_jaxpr/ppermute | solution.py:14
  22.7 6.8 %collective-permute-start = (bf16[48,24,222]{2,1,0:T(8,128)(2,1)S(1)}, bf16[48,24,222]{2,1,0:T(8,128)(2,1)S(1)}, u32[]{:S(2)}, u32[]{:S(2)}) collective-permute-start(bf16[48,24,222]{2,1,0:T(8,128)(2,1)S(1)} %get-tuple-element.307), channel_id=1, source_target_pairs={{0,504},{8,0},{16,8},{24,16},{32,24},{40,32},{48,40},{56,48},{64,5... | collective-permute-start | bytes 1534472 | tf_op jit(solution)/shard_map/while/body/eval_jaxpr/ppermute | solution.py:14
  29.5 7.7 %collective-permute-start.1 = (s32[48,24]{1,0:T(8,128)S(1)}, s32[48,24]{1,0:T(8,128)S(1)}, u32[]{:S(2)}, u32[]{:S(2)}) collective-permute-start(s32[48,24]{1,0:T(8,128)S(1)} %get-tuple-element.308), channel_id=1, source_target_pairs={{0,504},{8,0},{16,8},{24,16},{32,24},{40,32},{48,40},{56,48},{64,5... | collective-permute-start | bytes 13832 | tf_op jit(solution)/shard_map/while/body/eval_jaxpr/ppermute | solution.py:14
  39.6 6.8 %collective-permute-start = (bf16[48,24,222]{2,1,0:T(8,128)(2,1)S(1)}, bf16[48,24,222]{2,1,0:T(8,128)(2,1)S(1)}, u32[]{:S(2)}, u32[]{:S(2)}) collective-permute-start(bf16[48,24,222]{2,1,0:T(8,128)(2,1)S(1)} %get-tuple-element.307), channel_id=1, source_target_pairs={{0,504},{8,0},{16,8},{24,16},{32,24},{40,32},{48,40},{56,48},{64,5... | collective-permute-start | bytes 1534472 | tf_op jit(solution)/shard_map/while/body/eval_jaxpr/ppermute | solution.py:14
  46.4 7.7 %collective-permute-start.1 = (s32[48,24]{1,0:T(8,128)S(1)}, s32[48,24]{1,0:T(8,128)S(1)}, u32[]{:S(2)}, u32[]{:S(2)}) collective-permute-start(s32[48,24]{1,0:T(8,128)S(1)} %get-tuple-element.308), channel_id=1, source_target_pairs={{0,504},{8,0},{16,8},{24,16},{32,24},{40,32},{48,40},{56,48},{64,5... | collective-permute-start | bytes 13832 | tf_op jit(solution)/shard_map/while/body/eval_jaxpr/ppermute | solution.py:14
  56.5 6.8 %collective-permute-start = (bf16[48,24,222]{2,1,0:T(8,128)(2,1)S(1)}, bf16[48,24,222]{2,1,0:T(8,128)(2,1)S(1)}, u32[]{:S(2)}, u32[]{:S(2)}) collective-permute-start(bf16[48,24,222]{2,1,0:T(8,128)(2,1)S(1)} %get-tuple-element.307), channel_id=1, source_target_pairs={{0,504},{8,0},{16,8},{24,16},{32,24},{40,32},{48,40},{56,48},{64,5... | collective-permute-start | bytes 1534472 | tf_op jit(solution)/shard_map/while/body/eval_jaxpr/ppermute | solution.py:14
  63.3 7.7 %collective-permute-start.1 = (s32[48,24]{1,0:T(8,128)S(1)}, s32[48,24]{1,0:T(8,128)S(1)}, u32[]{:S(2)}, u32[]{:S(2)}) collective-permute-start(s32[48,24]{1,0:T(8,128)S(1)} %get-tuple-element.308), channel_id=1, source_target_pairs={{0,504},{8,0},{16,8},{24,16},{32,24},{40,32},{48,40},{56,48},{64,5... | collective-permute-start | bytes 13832 | tf_op jit(solution)/shard_map/while/body/eval_jaxpr/ppermute | solution.py:14
  73.4 6.8 %collective-permute-start = (bf16[48,24,222]{2,1,0:T(8,128)(2,1)S(1)}, bf16[48,24,222]{2,1,0:T(8,128)(2,1)S(1)}, u32[]{:S(2)}, u32[]{:S(2)}) collective-permute-start(bf16[48,24,222]{2,1,0:T(8,128)(2,1)S(1)} %get-tuple-element.307), channel_id=1, source_target_pairs={{0,504},{8,0},{16,8},{24,16},{32,24},{40,32},{48,40},{56,48},{64,5... | collective-permute-start | bytes 1534472 | tf_op jit(solution)/shard_map/while/body/eval_jaxpr/ppermute | solution.py:14
  80.2 7.7 %collective-permute-start.1 = (s32[48,24]{1,0:T(8,128)S(1)}, s32[48,24]{1,0:T(8,128)S(1)}, u32[]{:S(2)}, u32[]{:S(2)}) collective-permute-start(s32[48,24]{1,0:T(8,128)S(1)} %get-tuple-element.308), channel_id=1, source_target_pairs={{0,504},{8,0},{16,8},{24,16},{32,24},{40,32},{48,40},{56,48},{64,5... | collective-permute-start | bytes 13832 | tf_op jit(solution)/shard_map/while/body/eval_jaxpr/ppermute | solution.py:14
  90.2 6.8 %collective-permute-start = (bf16[48,24,222]{2,1,0:T(8,128)(2,1)S(1)}, bf16[48,24,222]{2,1,0:T(8,128)(2,1)S(1)}, u32[]{:S(2)}, u32[]{:S(2)}) collective-permute-start(bf16[48,24,222]{2,1,0:T(8,128)(2,1)S(1)} %get-tuple-element.307), channel_id=1, source_target_pairs={{0,504},{8,0},{16,8},{24,16},{32,24},{40,32},{48,40},{56,48},{64,5... | collective-permute-start | bytes 1534472 | tf_op jit(solution)/shard_map/while/body/eval_jaxpr/ppermute | solution.py:14
  97.0 7.7 %collective-permute-start.1 = (s32[48,24]{1,0:T(8,128)S(1)}, s32[48,24]{1,0:T(8,128)S(1)}, u32[]{:S(2)}, u32[]{:S(2)}) collective-permute-start(s32[48,24]{1,0:T(8,128)S(1)} %get-tuple-element.308), channel_id=1, source_target_pairs={{0,504},{8,0},{16,8},{24,16},{32,24},{40,32},{48,40},{56,48},{64,5... | collective-permute-start | bytes 13832 | tf_op jit(solution)/shard_map/while/body/eval_jaxpr/ppermute | solution.py:14
  107.0 6.8 %collective-permute-start = (bf16[48,24,222]{2,1,0:T(8,128)(2,1)S(1)}, bf16[48,24,222]{2,1,0:T(8,128)(2,1)S(1)}, u32[]{:S(2)}, u32[]{:S(2)}) collective-permute-start(bf16[48,24,222]{2,1,0:T(8,128)(2,1)S(1)} %get-tuple-element.307), channel_id=1, source_target_pairs={{0,504},{8,0},{16,8},{24,16},{32,24},{40,32},{48,40},{56,48},{64,5... | collective-permute-start | bytes 1534472 | tf_op jit(solution)/shard_map/while/body/eval_jaxpr/ppermute | solution.py:14
  113.8 7.7 %collective-permute-start.1 = (s32[48,24]{1,0:T(8,128)S(1)}, s32[48,24]{1,0:T(8,128)S(1)}, u32[]{:S(2)}, u32[]{:S(2)}) collective-permute-start(s32[48,24]{1,0:T(8,128)S(1)} %get-tuple-element.308), channel_id=1, source_target_pairs={{0,504},{8,0},{16,8},{24,16},{32,24},{40,32},{48,40},{56,48},{64,5... | collective-permute-start | bytes 13832 | tf_op jit(solution)/shard_map/while/body/eval_jaxpr/ppermute | solution.py:14
  123.9 6.8 %collective-permute-start = (bf16[48,24,222]{2,1,0:T(8,128)(2,1)S(1)}, bf16[48,24,222]{2,1,0:T(8,128)(2,1)S(1)}, u32[]{:S(2)}, u32[]{:S(2)}) collective-permute-start(bf16[48,24,222]{2,1,0:T(8,128)(2,1)S(1)} %get-tuple-element.307), channel_id=1, source_target_pairs={{0,504},{8,0},{16,8},{24,16},{32,24},{40,32},{48,40},{56,48},{64,5... | collective-permute-start | bytes 1534472 | tf_op jit(solution)/shard_map/while/body/eval_jaxpr/ppermute | solution.py:14
  130.7 7.7 %collective-permute-start.1 = (s32[48,24]{1,0:T(8,128)S(1)}, s32[48,24]{1,0:T(8,128)S(1)}, u32[]{:S(2)}, u32[]{:S(2)}) collective-permute-start(s32[48,24]{1,0:T(8,128)S(1)} %get-tuple-element.308), channel_id=1, source_target_pairs={{0,504},{8,0},{16,8},{24,16},{32,24},{40,32},{48,40},{56,48},{64,5... | collective-permute-start | bytes 13832 | tf_op jit(solution)/shard_map/while/body/eval_jaxpr/ppermute | solution.py:14
  140.8 6.8 %collective-permute-start = (bf16[48,24,222]{2,1,0:T(8,128)(2,1)S(1)}, bf16[48,24,222]{2,1,0:T(8,128)(2,1)S(1)}, u32[]{:S(2)}, u32[]{:S(2)}) collective-permute-start(bf16[48,24,222]{2,1,0:T(8,128)(2,1)S(1)} %get-tuple-element.307), channel_id=1, source_target_pairs={{0,504},{8,0},{16,8},{24,16},{32,24},{40,32},{48,40},{56,48},{64,5... | collective-permute-start | bytes 1534472 | tf_op jit(solution)/shard_map/while/body/eval_jaxpr/ppermute | solution.py:14
  147.6 7.7 %collective-permute-start.1 = (s32[48,24]{1,0:T(8,128)S(1)}, s32[48,24]{1,0:T(8,128)S(1)}, u32[]{:S(2)}, u32[]{:S(2)}) collective-permute-start(s32[48,24]{1,0:T(8,128)S(1)} %get-tuple-element.308), channel_id=1, source_target_pairs={{0,504},{8,0},{16,8},{24,16},{32,24},{40,32},{48,40},{56,48},{64,5... | collective-permute-start | bytes 13832 | tf_op jit(solution)/shard_map/while/body/eval_jaxpr/ppermute | solution.py:14
  157.7 6.8 %collective-permute-start = (bf16[48,24,222]{2,1,0:T(8,128)(2,1)S(1)}, bf16[48,24,222]{2,1,0:T(8,128)(2,1)S(1)}, u32[]{:S(2)}, u32[]{:S(2)}) collective-permute-start(bf16[48,24,222]{2,1,0:T(8,128)(2,1)S(1)} %get-tuple-element.307), channel_id=1, source_target_pairs={{0,504},{8,0},{16,8},{24,16},{32,24},{40,32},{48,40},{56,48},{64,5... | collective-permute-start | bytes 1534472 | tf_op jit(solution)/shard_map/while/body/eval_jaxpr/ppermute | solution.py:14
  164.5 7.7 %collective-permute-start.1 = (s32[48,24]{1,0:T(8,128)S(1)}, s32[48,24]{1,0:T(8,128)S(1)}, u32[]{:S(2)}, u32[]{:S(2)}) collective-permute-start(s32[48,24]{1,0:T(8,128)S(1)} %get-tuple-element.308), channel_id=1, source_target_pairs={{0,504},{8,0},{16,8},{24,16},{32,24},{40,32},{48,40},{56,48},{64,5... | collective-permute-start | bytes 13832 | tf_op jit(solution)/shard_map/while/body/eval_jaxpr/ppermute | solution.py:14
  174.5 6.8 %collective-permute-start = (bf16[48,24,222]{2,1,0:T(8,128)(2,1)S(1)}, bf16[48,24,222]{2,1,0:T(8,128)(2,1)S(1)}, u32[]{:S(2)}, u32[]{:S(2)}) collective-permute-start(bf16[48,24,222]{2,1,0:T(8,128)(2,1)S(1)} %get-tuple-element.307), channel_id=1, source_target_pairs={{0,504},{8,0},{16,8},{24,16},{32,24},{40,32},{48,40},{56,48},{64,5... | collective-permute-start | bytes 1534472 | tf_op jit(solution)/shard_map/while/body/eval_jaxpr/ppermute | solution.py:14
  181.3 7.7 %collective-permute-start.1 = (s32[48,24]{1,0:T(8,128)S(1)}, s32[48,24]{1,0:T(8,128)S(1)}, u32[]{:S(2)}, u32[]{:S(2)}) collective-permute-start(s32[48,24]{1,0:T(8,128)S(1)} %get-tuple-element.308), channel_id=1, source_target_pairs={{0,504},{8,0},{16,8},{24,16},{32,24},{40,32},{48,40},{56,48},{64,5... | collective-permute-start | bytes 13832 | tf_op jit(solution)/shard_map/while/body/eval_jaxpr/ppermute | solution.py:14
  191.3 6.8 %collective-permute-start = (bf16[48,24,222]{2,1,0:T(8,128)(2,1)S(1)}, bf16[48,24,222]{2,1,0:T(8,128)(2,1)S(1)}, u32[]{:S(2)}, u32[]{:S(2)}) collective-permute-start(bf16[48,24,222]{2,1,0:T(8,128)(2,1)S(1)} %get-tuple-element.307), channel_id=1, source_target_pairs={{0,504},{8,0},{16,8},{24,16},{32,24},{40,32},{48,40},{56,48},{64,5... | collective-permute-start | bytes 1534472 | tf_op jit(solution)/shard_map/while/body/eval_jaxpr/ppermute | solution.py:14
  198.1 7.7 %collective-permute-start.1 = (s32[48,24]{1,0:T(8,128)S(1)}, s32[48,24]{1,0:T(8,128)S(1)}, u32[]{:S(2)}, u32[]{:S(2)}) collective-permute-start(s32[48,24]{1,0:T(8,128)S(1)} %get-tuple-element.308), channel_id=1, source_target_pairs={{0,504},{8,0},{16,8},{24,16},{32,24},{40,32},{48,40},{56,48},{64,5... | collective-permute-start | bytes 13832 | tf_op jit(solution)/shard_map/while/body/eval_jaxpr/ppermute | solution.py:14
  208.0 6.8 %collective-permute-start = (bf16[48,24,222]{2,1,0:T(8,128)(2,1)S(1)}, bf16[48,24,222]{2,1,0:T(8,128)(2,1)S(1)}, u32[]{:S(2)}, u32[]{:S(2)}) collective-permute-start(bf16[48,24,222]{2,1,0:T(8,128)(2,1)S(1)} %get-tuple-element.307), channel_id=1, source_target_pairs={{0,504},{8,0},{16,8},{24,16},{32,24},{40,32},{48,40},{56,48},{64,5... | collective-permute-start | bytes 1534472 | tf_op jit(solution)/shard_map/while/body/eval_jaxpr/ppermute | solution.py:14
  214.8 7.7 %collective-permute-start.1 = (s32[48,24]{1,0:T(8,128)S(1)}, s32[48,24]{1,0:T(8,128)S(1)}, u32[]{:S(2)}, u32[]{:S(2)}) collective-permute-start(s32[48,24]{1,0:T(8,128)S(1)} %get-tuple-element.308), channel_id=1, source_target_pairs={{0,504},{8,0},{16,8},{24,16},{32,24},{40,32},{48,40},{56,48},{64,5... | collective-permute-start | bytes 13832 | tf_op jit(solution)/shard_map/while/body/eval_jaxpr/ppermute | solution.py:14
  224.7 6.8 %collective-permute-start = (bf16[48,24,222]{2,1,0:T(8,128)(2,1)S(1)}, bf16[48,24,222]{2,1,0:T(8,128)(2,1)S(1)}, u32[]{:S(2)}, u32[]{:S(2)}) collective-permute-start(bf16[48,24,222]{2,1,0:T(8,128)(2,1)S(1)} %get-tuple-element.307), channel_id=1, source_target_pairs={{0,504},{8,0},{16,8},{24,16},{32,24},{40,32},{48,40},{56,48},{64,5... | collective-permute-start | bytes 1534472 | tf_op jit(solution)/shard_map/while/body/eval_jaxpr/ppermute | solution.py:14
  231.5 7.7 %collective-permute-start.1 = (s32[48,24]{1,0:T(8,128)S(1)}, s32[48,24]{1,0:T(8,128)S(1)}, u32[]{:S(2)}, u32[]{:S(2)}) collective-permute-start(s32[48,24]{1,0:T(8,128)S(1)} %get-tuple-element.308), channel_id=1, source_target_pairs={{0,504},{8,0},{16,8},{24,16},{32,24},{40,32},{48,40},{56,48},{64,5... | collective-permute-start | bytes 13832 | tf_op jit(solution)/shard_map/while/body/eval_jaxpr/ppermute | solution.py:14
  241.5 35.2 %while.34 = (s32[]{:T(128)}, bf16[8,24,222]{2,1,0:T(8,128)(2,1)S(1)}, bf16[8,24,222]{2,1,0:T(8,128)(2,1)S(1)}, bf16[8,24,222]{2,1,0:T(8,128)(2,1)S(1)}, s32[8]{0...) while((s32[]{:T(128)}, ...), condition=%wide.region_6.7_spmd, body=%wide.region_2.6_spmd.sunk | while | flops 2288021 | bytes 1658771 | solution.py:83
  276.7 20.0 %all_to_all.5 = bf16[8,1,72,222]{3,2,1,0:T(8,128)(2,1)S(1)} all-to-all(bf16[8,1,72,222]{3,2,1,0:T(8,128)(2,1)S(1)} %maximum_bitcast_fusion), channel_id=1, replica_groups=mesh['lon'=64,'lat'=8] {'lat'}, dimensions={0} | all-to-all | bytes 511488 | tf_op jit(solution)/shard_map/all_to_all | solution.py:24
  (137 shorter events, 54.5 us)
Async XLA Ops:
  6.6 234.8 %copy-start = (s32[8]{0:T(128)S(1)}, s32[8]{0:T(128)}, u32[]{:S(2)}) copy-start(s32[8]{0:T(128)} %param.13) | copy-start | bytes 100
  6.6 15.1 %collective-permute-start = (bf16[48,24,222]{2,1,0:T(8,128)(2,1)S(1)}, bf16[48,24,222]{2,1,0:T(8,128)(2,1)S(1)}, u32[]{:S(2)}, u32[]{:S(2)}) collective-permute-start(bf16[48,24,222]{2,1,0:T(8,128)(2,1)S(1)} %get-tuple-element.307), channel_id=1, source_target_pairs={{0,504},{8,0},{16,8},{24,16},{32,24},{40,32},{48,40},{56,48},{64,5... | collective-permute-start | bytes 1534472 | tf_op jit(solution)/shard_map/while/body/eval_jaxpr/ppermute | solution.py:14
  15.5 5.7 %collective-permute-start.1 = (s32[48,24]{1,0:T(8,128)S(1)}, s32[48,24]{1,0:T(8,128)S(1)}, u32[]{:S(2)}, u32[]{:S(2)}) collective-permute-start(s32[48,24]{1,0:T(8,128)S(1)} %get-tuple-element.308), channel_id=1, source_target_pairs={{0,504},{8,0},{16,8},{24,16},{32,24},{40,32},{48,40},{56,48},{64,5... | collective-permute-start | bytes 13832 | tf_op jit(solution)/shard_map/while/body/eval_jaxpr/ppermute | solution.py:14
  22.7 15.9 %collective-permute-start = (bf16[48,24,222]{2,1,0:T(8,128)(2,1)S(1)}, bf16[48,24,222]{2,1,0:T(8,128)(2,1)S(1)}, u32[]{:S(2)}, u32[]{:S(2)}) collective-permute-start(bf16[48,24,222]{2,1,0:T(8,128)(2,1)S(1)} %get-tuple-element.307), channel_id=1, source_target_pairs={{0,504},{8,0},{16,8},{24,16},{32,24},{40,32},{48,40},{56,48},{64,5... | collective-permute-start | bytes 1534472 | tf_op jit(solution)/shard_map/while/body/eval_jaxpr/ppermute | solution.py:14
  29.5 8.6 %collective-permute-start.1 = (s32[48,24]{1,0:T(8,128)S(1)}, s32[48,24]{1,0:T(8,128)S(1)}, u32[]{:S(2)}, u32[]{:S(2)}) collective-permute-start(s32[48,24]{1,0:T(8,128)S(1)} %get-tuple-element.308), channel_id=1, source_target_pairs={{0,504},{8,0},{16,8},{24,16},{32,24},{40,32},{48,40},{56,48},{64,5... | collective-permute-start | bytes 13832 | tf_op jit(solution)/shard_map/while/body/eval_jaxpr/ppermute | solution.py:14
  39.6 15.9 %collective-permute-start = (bf16[48,24,222]{2,1,0:T(8,128)(2,1)S(1)}, bf16[48,24,222]{2,1,0:T(8,128)(2,1)S(1)}, u32[]{:S(2)}, u32[]{:S(2)}) collective-permute-start(bf16[48,24,222]{2,1,0:T(8,128)(2,1)S(1)} %get-tuple-element.307), channel_id=1, source_target_pairs={{0,504},{8,0},{16,8},{24,16},{32,24},{40,32},{48,40},{56,48},{64,5... | collective-permute-start | bytes 1534472 | tf_op jit(solution)/shard_map/while/body/eval_jaxpr/ppermute | solution.py:14
  46.4 8.6 %collective-permute-start.1 = (s32[48,24]{1,0:T(8,128)S(1)}, s32[48,24]{1,0:T(8,128)S(1)}, u32[]{:S(2)}, u32[]{:S(2)}) collective-permute-start(s32[48,24]{1,0:T(8,128)S(1)} %get-tuple-element.308), channel_id=1, source_target_pairs={{0,504},{8,0},{16,8},{24,16},{32,24},{40,32},{48,40},{56,48},{64,5... | collective-permute-start | bytes 13832 | tf_op jit(solution)/shard_map/while/body/eval_jaxpr/ppermute | solution.py:14
  56.5 15.9 %collective-permute-start = (bf16[48,24,222]{2,1,0:T(8,128)(2,1)S(1)}, bf16[48,24,222]{2,1,0:T(8,128)(2,1)S(1)}, u32[]{:S(2)}, u32[]{:S(2)}) collective-permute-start(bf16[48,24,222]{2,1,0:T(8,128)(2,1)S(1)} %get-tuple-element.307), channel_id=1, source_target_pairs={{0,504},{8,0},{16,8},{24,16},{32,24},{40,32},{48,40},{56,48},{64,5... | collective-permute-start | bytes 1534472 | tf_op jit(solution)/shard_map/while/body/eval_jaxpr/ppermute | solution.py:14
  63.3 8.6 %collective-permute-start.1 = (s32[48,24]{1,0:T(8,128)S(1)}, s32[48,24]{1,0:T(8,128)S(1)}, u32[]{:S(2)}, u32[]{:S(2)}) collective-permute-start(s32[48,24]{1,0:T(8,128)S(1)} %get-tuple-element.308), channel_id=1, source_target_pairs={{0,504},{8,0},{16,8},{24,16},{32,24},{40,32},{48,40},{56,48},{64,5... | collective-permute-start | bytes 13832 | tf_op jit(solution)/shard_map/while/body/eval_jaxpr/ppermute | solution.py:14
  73.4 15.9 %collective-permute-start = (bf16[48,24,222]{2,1,0:T(8,128)(2,1)S(1)}, bf16[48,24,222]{2,1,0:T(8,128)(2,1)S(1)}, u32[]{:S(2)}, u32[]{:S(2)}) collective-permute-start(bf16[48,24,222]{2,1,0:T(8,128)(2,1)S(1)} %get-tuple-element.307), channel_id=1, source_target_pairs={{0,504},{8,0},{16,8},{24,16},{32,24},{40,32},{48,40},{56,48},{64,5... | collective-permute-start | bytes 1534472 | tf_op jit(solution)/shard_map/while/body/eval_jaxpr/ppermute | solution.py:14
  80.2 8.6 %collective-permute-start.1 = (s32[48,24]{1,0:T(8,128)S(1)}, s32[48,24]{1,0:T(8,128)S(1)}, u32[]{:S(2)}, u32[]{:S(2)}) collective-permute-start(s32[48,24]{1,0:T(8,128)S(1)} %get-tuple-element.308), channel_id=1, source_target_pairs={{0,504},{8,0},{16,8},{24,16},{32,24},{40,32},{48,40},{56,48},{64,5... | collective-permute-start | bytes 13832 | tf_op jit(solution)/shard_map/while/body/eval_jaxpr/ppermute | solution.py:14
  90.2 15.9 %collective-permute-start = (bf16[48,24,222]{2,1,0:T(8,128)(2,1)S(1)}, bf16[48,24,222]{2,1,0:T(8,128)(2,1)S(1)}, u32[]{:S(2)}, u32[]{:S(2)}) collective-permute-start(bf16[48,24,222]{2,1,0:T(8,128)(2,1)S(1)} %get-tuple-element.307), channel_id=1, source_target_pairs={{0,504},{8,0},{16,8},{24,16},{32,24},{40,32},{48,40},{56,48},{64,5... | collective-permute-start | bytes 1534472 | tf_op jit(solution)/shard_map/while/body/eval_jaxpr/ppermute | solution.py:14
  97.0 8.6 %collective-permute-start.1 = (s32[48,24]{1,0:T(8,128)S(1)}, s32[48,24]{1,0:T(8,128)S(1)}, u32[]{:S(2)}, u32[]{:S(2)}) collective-permute-start(s32[48,24]{1,0:T(8,128)S(1)} %get-tuple-element.308), channel_id=1, source_target_pairs={{0,504},{8,0},{16,8},{24,16},{32,24},{40,32},{48,40},{56,48},{64,5... | collective-permute-start | bytes 13832 | tf_op jit(solution)/shard_map/while/body/eval_jaxpr/ppermute | solution.py:14
  107.0 15.9 %collective-permute-start = (bf16[48,24,222]{2,1,0:T(8,128)(2,1)S(1)}, bf16[48,24,222]{2,1,0:T(8,128)(2,1)S(1)}, u32[]{:S(2)}, u32[]{:S(2)}) collective-permute-start(bf16[48,24,222]{2,1,0:T(8,128)(2,1)S(1)} %get-tuple-element.307), channel_id=1, source_target_pairs={{0,504},{8,0},{16,8},{24,16},{32,24},{40,32},{48,40},{56,48},{64,5... | collective-permute-start | bytes 1534472 | tf_op jit(solution)/shard_map/while/body/eval_jaxpr/ppermute | solution.py:14
  113.8 8.6 %collective-permute-start.1 = (s32[48,24]{1,0:T(8,128)S(1)}, s32[48,24]{1,0:T(8,128)S(1)}, u32[]{:S(2)}, u32[]{:S(2)}) collective-permute-start(s32[48,24]{1,0:T(8,128)S(1)} %get-tuple-element.308), channel_id=1, source_target_pairs={{0,504},{8,0},{16,8},{24,16},{32,24},{40,32},{48,40},{56,48},{64,5... | collective-permute-start | bytes 13832 | tf_op jit(solution)/shard_map/while/body/eval_jaxpr/ppermute | solution.py:14
  123.9 15.9 %collective-permute-start = (bf16[48,24,222]{2,1,0:T(8,128)(2,1)S(1)}, bf16[48,24,222]{2,1,0:T(8,128)(2,1)S(1)}, u32[]{:S(2)}, u32[]{:S(2)}) collective-permute-start(bf16[48,24,222]{2,1,0:T(8,128)(2,1)S(1)} %get-tuple-element.307), channel_id=1, source_target_pairs={{0,504},{8,0},{16,8},{24,16},{32,24},{40,32},{48,40},{56,48},{64,5... | collective-permute-start | bytes 1534472 | tf_op jit(solution)/shard_map/while/body/eval_jaxpr/ppermute | solution.py:14
  130.7 8.6 %collective-permute-start.1 = (s32[48,24]{1,0:T(8,128)S(1)}, s32[48,24]{1,0:T(8,128)S(1)}, u32[]{:S(2)}, u32[]{:S(2)}) collective-permute-start(s32[48,24]{1,0:T(8,128)S(1)} %get-tuple-element.308), channel_id=1, source_target_pairs={{0,504},{8,0},{16,8},{24,16},{32,24},{40,32},{48,40},{56,48},{64,5... | collective-permute-start | bytes 13832 | tf_op jit(solution)/shard_map/while/body/eval_jaxpr/ppermute | solution.py:14
  140.8 15.9 %collective-permute-start = (bf16[48,24,222]{2,1,0:T(8,128)(2,1)S(1)}, bf16[48,24,222]{2,1,0:T(8,128)(2,1)S(1)}, u32[]{:S(2)}, u32[]{:S(2)}) collective-permute-start(bf16[48,24,222]{2,1,0:T(8,128)(2,1)S(1)} %get-tuple-element.307), channel_id=1, source_target_pairs={{0,504},{8,0},{16,8},{24,16},{32,24},{40,32},{48,40},{56,48},{64,5... | collective-permute-start | bytes 1534472 | tf_op jit(solution)/shard_map/while/body/eval_jaxpr/ppermute | solution.py:14
  147.6 8.6 %collective-permute-start.1 = (s32[48,24]{1,0:T(8,128)S(1)}, s32[48,24]{1,0:T(8,128)S(1)}, u32[]{:S(2)}, u32[]{:S(2)}) collective-permute-start(s32[48,24]{1,0:T(8,128)S(1)} %get-tuple-element.308), channel_id=1, source_target_pairs={{0,504},{8,0},{16,8},{24,16},{32,24},{40,32},{48,40},{56,48},{64,5... | collective-permute-start | bytes 13832 | tf_op jit(solution)/shard_map/while/body/eval_jaxpr/ppermute | solution.py:14
  157.7 15.9 %collective-permute-start = (bf16[48,24,222]{2,1,0:T(8,128)(2,1)S(1)}, bf16[48,24,222]{2,1,0:T(8,128)(2,1)S(1)}, u32[]{:S(2)}, u32[]{:S(2)}) collective-permute-start(bf16[48,24,222]{2,1,0:T(8,128)(2,1)S(1)} %get-tuple-element.307), channel_id=1, source_target_pairs={{0,504},{8,0},{16,8},{24,16},{32,24},{40,32},{48,40},{56,48},{64,5... | collective-permute-start | bytes 1534472 | tf_op jit(solution)/shard_map/while/body/eval_jaxpr/ppermute | solution.py:14
  164.5 8.6 %collective-permute-start.1 = (s32[48,24]{1,0:T(8,128)S(1)}, s32[48,24]{1,0:T(8,128)S(1)}, u32[]{:S(2)}, u32[]{:S(2)}) collective-permute-start(s32[48,24]{1,0:T(8,128)S(1)} %get-tuple-element.308), channel_id=1, source_target_pairs={{0,504},{8,0},{16,8},{24,16},{32,24},{40,32},{48,40},{56,48},{64,5... | collective-permute-start | bytes 13832 | tf_op jit(solution)/shard_map/while/body/eval_jaxpr/ppermute | solution.py:14
  174.5 15.8 %collective-permute-start = (bf16[48,24,222]{2,1,0:T(8,128)(2,1)S(1)}, bf16[48,24,222]{2,1,0:T(8,128)(2,1)S(1)}, u32[]{:S(2)}, u32[]{:S(2)}) collective-permute-start(bf16[48,24,222]{2,1,0:T(8,128)(2,1)S(1)} %get-tuple-element.307), channel_id=1, source_target_pairs={{0,504},{8,0},{16,8},{24,16},{32,24},{40,32},{48,40},{56,48},{64,5... | collective-permute-start | bytes 1534472 | tf_op jit(solution)/shard_map/while/body/eval_jaxpr/ppermute | solution.py:14
  181.3 8.6 %collective-permute-start.1 = (s32[48,24]{1,0:T(8,128)S(1)}, s32[48,24]{1,0:T(8,128)S(1)}, u32[]{:S(2)}, u32[]{:S(2)}) collective-permute-start(s32[48,24]{1,0:T(8,128)S(1)} %get-tuple-element.308), channel_id=1, source_target_pairs={{0,504},{8,0},{16,8},{24,16},{32,24},{40,32},{48,40},{56,48},{64,5... | collective-permute-start | bytes 13832 | tf_op jit(solution)/shard_map/while/body/eval_jaxpr/ppermute | solution.py:14
  191.3 15.8 %collective-permute-start = (bf16[48,24,222]{2,1,0:T(8,128)(2,1)S(1)}, bf16[48,24,222]{2,1,0:T(8,128)(2,1)S(1)}, u32[]{:S(2)}, u32[]{:S(2)}) collective-permute-start(bf16[48,24,222]{2,1,0:T(8,128)(2,1)S(1)} %get-tuple-element.307), channel_id=1, source_target_pairs={{0,504},{8,0},{16,8},{24,16},{32,24},{40,32},{48,40},{56,48},{64,5... | collective-permute-start | bytes 1534472 | tf_op jit(solution)/shard_map/while/body/eval_jaxpr/ppermute | solution.py:14
  198.1 8.6 %collective-permute-start.1 = (s32[48,24]{1,0:T(8,128)S(1)}, s32[48,24]{1,0:T(8,128)S(1)}, u32[]{:S(2)}, u32[]{:S(2)}) collective-permute-start(s32[48,24]{1,0:T(8,128)S(1)} %get-tuple-element.308), channel_id=1, source_target_pairs={{0,504},{8,0},{16,8},{24,16},{32,24},{40,32},{48,40},{56,48},{64,5... | collective-permute-start | bytes 13832 | tf_op jit(solution)/shard_map/while/body/eval_jaxpr/ppermute | solution.py:14
  208.0 15.8 %collective-permute-start = (bf16[48,24,222]{2,1,0:T(8,128)(2,1)S(1)}, bf16[48,24,222]{2,1,0:T(8,128)(2,1)S(1)}, u32[]{:S(2)}, u32[]{:S(2)}) collective-permute-start(bf16[48,24,222]{2,1,0:T(8,128)(2,1)S(1)} %get-tuple-element.307), channel_id=1, source_target_pairs={{0,504},{8,0},{16,8},{24,16},{32,24},{40,32},{48,40},{56,48},{64,5... | collective-permute-start | bytes 1534472 | tf_op jit(solution)/shard_map/while/body/eval_jaxpr/ppermute | solution.py:14
  214.8 8.6 %collective-permute-start.1 = (s32[48,24]{1,0:T(8,128)S(1)}, s32[48,24]{1,0:T(8,128)S(1)}, u32[]{:S(2)}, u32[]{:S(2)}) collective-permute-start(s32[48,24]{1,0:T(8,128)S(1)} %get-tuple-element.308), channel_id=1, source_target_pairs={{0,504},{8,0},{16,8},{24,16},{32,24},{40,32},{48,40},{56,48},{64,5... | collective-permute-start | bytes 13832 | tf_op jit(solution)/shard_map/while/body/eval_jaxpr/ppermute | solution.py:14
  224.7 15.8 %collective-permute-start = (bf16[48,24,222]{2,1,0:T(8,128)(2,1)S(1)}, bf16[48,24,222]{2,1,0:T(8,128)(2,1)S(1)}, u32[]{:S(2)}, u32[]{:S(2)}) collective-permute-start(bf16[48,24,222]{2,1,0:T(8,128)(2,1)S(1)} %get-tuple-element.307), channel_id=1, source_target_pairs={{0,504},{8,0},{16,8},{24,16},{32,24},{40,32},{48,40},{56,48},{64,5... | collective-permute-start | bytes 1534472 | tf_op jit(solution)/shard_map/while/body/eval_jaxpr/ppermute | solution.py:14
  231.5 8.6 %collective-permute-start.1 = (s32[48,24]{1,0:T(8,128)S(1)}, s32[48,24]{1,0:T(8,128)S(1)}, u32[]{:S(2)}, u32[]{:S(2)}) collective-permute-start(s32[48,24]{1,0:T(8,128)S(1)} %get-tuple-element.308), channel_id=1, source_target_pairs={{0,504},{8,0},{16,8},{24,16},{32,24},{40,32},{48,40},{56,48},{64,5... | collective-permute-start | bytes 13832 | tf_op jit(solution)/shard_map/while/body/eval_jaxpr/ppermute | solution.py:14
where the time goes:
time: 303 us; the launch traced here: 297 us
  starting transfers between devices  203 us (67%)
  local copies, waits for them, and re-layouts  30.3 us (10%)
  blocking collectives  20 us (7%)
  other arithmetic  16.7 us (6%)
  loops' own time  16.3 us (5%)
  waiting for transfers between devices  11.5 us (4%)
    ppermute x28, starting transfers between devices, from_behind(): lax.ppermute(value, axis, [(i, (i + by) % count) for i in range(count)])  203 us
    all_to_all x1, blocking collectives, sent_and_summed(): lax.all_to_all(in_blocks(value, dim, count), axis, 0, 0, tiled=True)  20 us
    another operation x1, loops' own time, local(): lax.map(lag_sums, eastward_offsets)  15.6 us
    reduce_sum x8, other arithmetic, lag_sums(): var_true = jnp.sum(couple_factor * frame_segment * frame_segment, axis=0)  13.6 us
    dynamic_update_slice x14, local copies, waits for them, and re-layouts, advance(): lax.dynamic_update_slice_in_dim(buffer_true, slab_true, place, 1)  12.7 us
    ppermute x28, waiting for transfers between devices, from_behind(): lax.ppermute(value, axis, [(i, (i + by) % count) for i in range(count)])  11.5 us
    dynamic_update_slice x14, local copies, waits for them, and re-layouts, advance(): lax.dynamic_update_slice_in_dim(buffer_valid, slab_valid, place, 1)  6.75 us
  transfers between devices with their start and end apart: 28, of which 14 were waited for; matrix products, arithmetic and copies ran while one was open for 2% of the time, Pallas kernels for 0%

commit v1 on v0

v1 whole, which is shorter than its diff:
```python
import functools

import jax
import jax.numpy as jnp
import numpy as np
from jax import lax
from jax.experimental import pallas as pl
from jax.experimental.pallas import tpu as pltpu
from jax.sharding import Mesh
from jax.sharding import PartitionSpec as P

REG = 0.001
K = 8
ROWS = 48
COLS = 24
CHANNELS = 222
GROUPS = 16
PER = 14
SLOT = 16
SUB = 8
STEPS = ROWS // SUB
BLOCK = GROUPS * COLS
HALO = 14
WINDOW = BLOCK + HALO * COLS
MISSING = 1024.0
LANES = 128


def pack_kernel(field_ref, mean_ref, flags_ref, out_ref, low, mid, high):
    step = pl.program_id(0)
    lane = lax.broadcasted_iota(jnp.int32, (COLS, LANES), 1)
    flags = flags_ref[pl.ds(pl.multiple_of(step * SUB, SUB), SUB), :]
    valid = flags.astype(jnp.float32).T
    pad = jnp.zeros((COLS, 2 * LANES - CHANNELS), jnp.float32)
    for r in range(SUB):
        keep = jnp.broadcast_to(valid[:, r : r + 1], (COLS, LANES)) > 0.5
        left = field_ref[r, :, :LANES].astype(jnp.float32) - mean_ref[r, :, :LANES].astype(jnp.float32)
        right = field_ref[r, :, LANES:].astype(jnp.float32) - mean_ref[r, :, LANES:].astype(jnp.float32)
        left = jnp.where(keep, left, MISSING)
        right = jnp.where(keep, jnp.concatenate([right, pad], axis=1), MISSING)
        low[r] = left
        high[r] = right
        mid[r] = jnp.where(lane >= 9 * PER, left, right)
    for q in range(GROUPS):
        source = low if q < 9 else mid if q == 9 else high
        acc = jnp.full((COLS, LANES), MISSING, jnp.float32)
        for r in range(SUB):
            moved = pltpu.roll(source[r], (SLOT * r - PER * q) % LANES, 1)
            here = (lane >= SLOT * r) & (lane < SLOT * r + PER)
            acc = jnp.where(here, moved, acc)
        out_ref[q] = acc.astype(jnp.bfloat16)


def pack(field, mean, flags):
    return pl.pallas_call(
        pack_kernel,
        grid=(STEPS,),
        in_specs=[
            pl.BlockSpec((SUB, COLS, CHANNELS), lambda i: (i, 0, 0)),
            pl.BlockSpec((SUB, COLS, CHANNELS), lambda i: (i, 0, 0)),
            pl.BlockSpec((ROWS, COLS), lambda i: (0, 0)),
        ],
        out_specs=pl.BlockSpec((GROUPS, COLS, LANES), lambda i: (0, i, 0)),
        out_shape=jax.ShapeDtypeStruct((GROUPS, STEPS * COLS, LANES), jnp.bfloat16),
        scratch_shapes=[pltpu.VMEM((SUB, COLS, LANES), jnp.float32)] * 3,
        cost_estimate=pl.CostEstimate(flops=4_000_000, bytes_accessed=2_000_000, transcendentals=0),
        name="pack",
    )(field, mean, flags)


def sums_kernel(offsets_ref, weight_ref, fore_ref, true_ref, next_ref, gather_ref, out_ref, cross, square, weigh, shifted, usable, total):
    for g in range(STEPS):
        weight = weight_ref[g : g + 1, :]
        rows = pl.ds(g * COLS, COLS)

        def own(p, carry):
            at = pl.ds(pl.multiple_of(g * BLOCK + p * COLS, 8), COLS)
            value = fore_ref[p, rows, :].astype(jnp.float32)
            keep = value < MISSING / 2
            value = jnp.where(keep, value, 0.0)
            masked = jnp.where(keep, weight, 0.0)
            weigh[at, :] = masked
            scaled = value * masked
            cross[at, :] = scaled
            square[at, :] = scaled * value
            return carry

        lax.fori_loop(0, GROUPS, own, 0)

        def other(source, first):
            def run(p, carry):
                at = pl.ds(pl.multiple_of(g * WINDOW + first + p * COLS, 8), COLS)
                value = source[p, rows, :].astype(jnp.float32)
                keep = value < MISSING / 2
                shifted[at, :] = jnp.where(keep, value, 0.0)
                usable[at, :] = jnp.where(keep, 1.0, 0.0)
                return carry

            return run

        lax.fori_loop(0, GROUPS, other(true_ref, 0), 0)
        lax.fori_loop(0, HALO, other(next_ref, BLOCK), 0)

    lag = [offsets_ref[k] for k in range(K)]

    def tile(t, carry):
        for part in range(COLS // 8):
            start = t * COLS + part * 8
            acc = [[jnp.zeros((8, LANES), jnp.float32)] * 3 for _ in range(K)]
            for g in range(STEPS):
                at = pl.ds(pl.multiple_of(g * BLOCK + start, 8), 8)
                a, c, d = cross[at, :], square[at, :], weigh[at, :]
                for k in range(K):
                    there = pl.ds(g * WINDOW + start + lag[k], 8)
                    b, v = shifted[there, :], usable[there, :]
                    acc[k] = [acc[k][0] + a * b, acc[k][1] + c * v, acc[k][2] + d * (b * b)]
            for k in range(K):
                for n in range(3):
                    column = (n * 3 + part) * LANES
                    total[pl.ds(pl.multiple_of((k * GROUPS + t) * 8, 8), 8), column : column + LANES] = acc[k][n]
        return carry

    lax.fori_loop(0, GROUPS, tile, 0)
    whole = total[...]
    first = whole.astype(jnp.bfloat16)
    second = (whole - first.astype(jnp.float32)).astype(jnp.bfloat16)
    gather = gather_ref[...]
    out = jnp.dot(first, gather, preferred_element_type=jnp.float32)
    out += jnp.dot(second, gather, preferred_element_type=jnp.float32)
    out_ref[...] = out.astype(jnp.bfloat16)


def gather_matrix():
    m = np.zeros((9, SUB, SLOT, LANES), np.float32)
    for n in range(9):
        for c in range(PER):
            m[n, :, c, n * PER + c] = 1.0
    return m.reshape(9 * LANES, LANES)


def lag_sums(offsets, weight, fore, true, following):
    vmem = pl.BlockSpec(memory_space=pltpu.VMEM)
    f32 = jnp.float32
    return pl.pallas_call(
        sums_kernel,
        in_specs=[pl.BlockSpec(memory_space=pltpu.SMEM)] + [vmem] * 5,
        out_specs=vmem,
        out_shape=jax.ShapeDtypeStruct((K * GROUPS * 8, LANES), jnp.bfloat16),
        scratch_shapes=[pltpu.VMEM((STEPS * BLOCK, LANES), f32)] * 3
        + [pltpu.VMEM((STEPS * WINDOW, LANES), f32)] * 2
        + [pltpu.VMEM((K * GROUPS * 8, 9 * LANES), f32)],
        cost_estimate=pl.CostEstimate(flops=20_000_000, bytes_accessed=4_000_000, transcendentals=0),
        name="lag_sums",
    )(offsets, weight, fore, true, following, jnp.asarray(gather_matrix(), jnp.bfloat16))


def finish_kernel(parts_ref, out_ref):
    lane = lax.broadcasted_iota(jnp.int32, (8, LANES), 1)
    halves = [[jnp.zeros((8, LANES), jnp.float32)] * 2 for _ in range(3)]
    for q in range(GROUPS):
        total = parts_ref[q].astype(jnp.float32)
        for device in range(1, K):
            total = total + parts_ref[device * GROUPS + q].astype(jnp.float32)
        fore = pltpu.roll(total, LANES - 3 * PER, 1)
        true = pltpu.roll(total, LANES - 6 * PER, 1)
        value = total / jnp.sqrt((fore + REG) * (true + REG))
        low, high = PER * q, PER * q + PER
        for part in range(3):
            moved = pltpu.roll(value, (PER * q - PER * part) % LANES, 1)
            for half in range(2):
                at = lane + half * LANES
                if low < (half + 1) * LANES and high > half * LANES:
                    halves[part][half] = jnp.where((at >= low) & (at < high), moved, halves[part][half])
    for part in range(3):
        out_ref[0, part * 8 : part * 8 + 8, :LANES] = halves[part][0]
        out_ref[0, part * 8 : part * 8 + 8, LANES:] = halves[part][1][:, : CHANNELS - LANES]


def finish(parts):
    vmem = pl.BlockSpec(memory_space=pltpu.VMEM)
    return pl.pallas_call(
        finish_kernel,
        in_specs=[vmem],
        out_specs=vmem,
        out_shape=jax.ShapeDtypeStruct((1, COLS, CHANNELS), jnp.float32),
        name="finish",
    )(parts)


def local(prediction, observed_state, mean_state, usable_point_flags, eastward_offsets):
    row = lax.axis_index("lat") * ROWS + jnp.arange(ROWS, dtype=jnp.int32)
    weight = jnp.cos(jnp.pi * ((row.astype(jnp.float32) + 0.5) / (ROWS * lax.axis_size("lat")) - 0.5))
    weight = jnp.repeat(weight.reshape(STEPS, SUB), SLOT, axis=1)
    around = ("y", "core")
    true = pack(observed_state, mean_state, usable_point_flags)
    true = lax.all_to_all(true, around, 0, 0, tiled=True)
    count = lax.axis_size("z")
    following = lax.ppermute(true[:HALO], "z", [((i + 1) % count, i) for i in range(count)])
    fore = pack(prediction, mean_state, usable_point_flags)
    fore = lax.all_to_all(fore, around, 0, 0, tiled=True)
    sums = lag_sums(eastward_offsets, weight, fore, true, following)
    parts = sums.reshape(K * GROUPS, 8, LANES)
    parts = lax.all_to_all(parts, ("lat",) + around, 0, 0, tiled=True)
    return finish(parts)


def solution(mesh):
    split = Mesh(mesh.devices.reshape(4, 8, 2, 8), ("z", "y", "core", "lat"))
    lon = ("z", "y", "core")
    placed = (P("lat", lon, None), P("lat", lon, None), P("lat", lon, None), P("lat", lon), P())
    return jax.shard_map(local, mesh=split, in_specs=placed, out_specs=P("lat", lon, None), check_vma=False)
```

time: 303 us -> 104 us (0.34); the launches traced: 297 us -> 103 us
  starting transfers between devices: 203 us -> 19.5 us
  local copies, waits for them, and re-layouts: 30.3 us -> 3.83 us
  Pallas kernels: 0 us -> 21.3 us
  other arithmetic: 16.7 us -> 0.05 us
  loops' own time: 16.3 us -> 0 us
  blocking collectives: 20 us -> 33.5 us
  waiting for transfers between devices: 11.5 us -> 24.4 us
    ppermute x28 -> x1, starting transfers between devices: 203 us -> 5.84 us  [local(): lax.ppermute(true[:HALO], 'z', [((i + 1) % count, i) for i in range(count)])]
    all_to_all x0 -> x2, waiting for transfers between devices: none -> 24.4 us  [the longest x1 13.1 us: local(): true = lax.all_to_all(true, around, 0, 0, tiled=True)]
    dynamic_update_slice x46 -> x0, local copies, waits for them, and re-layouts: 23.7 us -> none  [the longest x14 12.7 us: advance(): lax.dynamic_update_slice_in_dim(buffer_true, slab_true, place, 1)]
    pallas_call x0 -> x4, Pallas kernels: none -> 21.3 us  [the longest x2 11.2 us: pack(): pl.pallas_call(pack_kernel, grid=(STEPS,), in_specs=[pl.BlockSpec((SUB, C...]
    another operation x2 -> x0, loops' own time: 16.3 us -> none  [the longest x1 15.6 us: local(): lax.map(lag_sums, eastward_offsets)]
    all_to_all x0 -> x2, starting transfers between devices: none -> 13.7 us  [the longest x1 10.2 us: local(): true = lax.all_to_all(true, around, 0, 0, tiled=True)]
    reduce_sum x9 -> x0, other arithmetic: 13.7 us -> none  [the longest x8 13.6 us: lag_sums(): var_true = jnp.sum(couple_factor * frame_segment * frame_segment, axis=0)]
    all_to_all x1, blocking collectives: 20 us -> 33.5 us  [local(): parts = lax.all_to_all(parts, ('lat',) + around, 0, 0, tiled=True)]
  transfers between devices with their start and end apart: 28 -> 3, of which waited for: 14 -> 2; matrix products, arithmetic and copies ran while one was open for 2% -> 1% of each run, Pallas kernels for 0% -> 5%
where the time goes in v1:
time: 104 us; the launch traced here: 103 us
  blocking collectives  33.5 us (32%)
  waiting for transfers between devices  24.4 us (23%)
  Pallas kernels  21.3 us (20%)
  starting transfers between devices  19.5 us (19%)
  local copies, waits for them, and re-layouts  3.83 us (4%)
    all_to_all x1, blocking collectives, local(): parts = lax.all_to_all(parts, ('lat',) + around, 0, 0, tiled=True)  33.5 us
    all_to_all x1, waiting for transfers between devices, local(): true = lax.all_to_all(true, around, 0, 0, tiled=True)  13.1 us
    all_to_all x1, waiting for transfers between devices, local(): fore = lax.all_to_all(fore, around, 0, 0, tiled=True)  11.3 us
    pallas_call x2, Pallas kernels, pack(): pl.pallas_call(pack_kernel, grid=(STEPS,), in_specs=[pl.BlockSpec((SUB, C...  11.2 us
    all_to_all x1, starting transfers between devices, local(): true = lax.all_to_all(true, around, 0, 0, tiled=True)  10.2 us
    pallas_call x1, Pallas kernels, lag_sums(): pl.pallas_call(sums_kernel, in_specs=[pl.BlockSpec(memory_space=pltpu.SME...  8.39 us
    ppermute x1, starting transfers between devices, local(): lax.ppermute(true[:HALO], 'z', [((i + 1) % count, i) for i in range(count)])  5.84 us
    all_to_all x1, starting transfers between devices, local(): fore = lax.all_to_all(fore, around, 0, 0, tiled=True)  3.48 us
  transfers between devices with their start and end apart: 3, of which 2 were waited for; matrix products, arithmetic and copies ran while one was open for 1% of the time, Pallas kernels for 5%

profile of v1, /device:TPU:1, one launch (start us, length us, event | category | flops | bytes accessed | tf_op | source)
XLA Modules:
  0.0 102.8 jit_solution(17039472812025788355)
XLA Ops:
  0.0 1.4 %copy.7.flags_ref = s32[48,24]{1,0:T(8,128)} copy(s32[48,24]{0,1:T(8,128)} %param.9) | data formatting | bytes 9216 | tf_op args[3]
  1.4 5.6 %pack.3 = bf16[16,144,128]{2,1,0:T(8,128)(2,1)} custom-call(bf16[48,24,222]{2,1,0:T(8,128)(2,1)} %field_ref.3, bf16[48,24,222]{2,1,0:T(8,128)(2,1)} %mean_ref.3, s32[48,24]{1,0:T(8,128)} %copy.7.flags_ref), custom_call_target="tpu_custom_call" | custom-call | flops 4000000 | bytes 2000000 | tf_op jit(solution)/shard_map/pack/pallas_call | solution.py:55
  7.0 10.2 %all-to-all-start.1 = ((bf16[16,144,128]{2,1,0:T(8,128)(2,1)}), bf16[16,144,128]{2,1,0:T(8,128)(2,1)S(1)}, u32[]{:S(2)}, u32[]{:S(2)}) async-start(bf16[16,144,128]{2,1,0:T(8,128)(2,1)} %pack.3), calls=%async_computation.1 | async-start | bytes 1179648 | tf_op jit(solution)/shard_map/all_to_all | solution.py:196
  17.2 5.6 %pack.2 = bf16[16,144,128]{2,1,0:T(8,128)(2,1)} custom-call(bf16[48,24,222]{2,1,0:T(8,128)(2,1)} %field_ref.2, bf16[48,24,222]{2,1,0:T(8,128)(2,1)} %mean_ref.3, s32[48,24]{1,0:T(8,128)} %copy.7.flags_ref), custom_call_target="tpu_custom_call" | custom-call | flops 4000000 | bytes 2000000 | tf_op jit(solution)/shard_map/pack/pallas_call | solution.py:55
  22.8 13.1 %all-to-all-done.1.true_ref = bf16[16,144,128]{2,1,0:T(8,128)(2,1)S(1)} async-done(((bf16[16,144,128]{2,1,0:T(8,128)(2,1)}), bf16[16,144,128]{2,1,0:T(8,128)(2,1)S(1)}, u32[]{:S(2)}, u32[]{:S(2)}) %all-to-all-start.1) | async-done | bytes 589856 | tf_op jit(solution)/shard_map/all_to_all | solution.py:196
  35.9 0.0 copy-start
  35.9 3.5 %all-to-all-start = ((bf16[16,144,128]{2,1,0:T(8,128)(2,1)}), bf16[16,144,128]{2,1,0:T(8,128)(2,1)S(1)}, u32[]{:S(2)}, u32[]{:S(2)}) async-start(bf16[16,144,128]{2,1,0:T(8,128)(2,1)} %pack.2), calls=%async_computation | async-start | bytes 1179648 | tf_op jit(solution)/shard_map/all_to_all | solution.py:200
  39.4 0.0 copy-done
  39.5 5.8 %collective-permute-start = (bf16[14,144,128]{2,1,0:T(8,128)(2,1)S(1)}, bf16[14,144,128]{2,1,0:T(8,128)(2,1)S(1)}, u32[]{:S(2)}, u32[]{:S(2)}) collective-permute-start(bf16[14,144,128]{2,1,0:T(8,128)(2,1)S(1)} %slice.4), channel_id=1, source_target_pairs={{128,0},{256,128},{384,256},{0,384},{129,1},{257,129},{385,257},{1... | collective-permute-start | bytes 1548296 | tf_op jit(solution)/shard_map/ppermute | solution.py:198
  45.3 0.1 multiply_cosine_fusion
  45.4 0.1 broadcast_in_dim.3
  45.4 0.7 reshape.8.weight_ref
  46.1 11.3 %all-to-all-done.fore_ref = bf16[16,144,128]{2,1,0:T(8,128)(2,1)S(1)} async-done(((bf16[16,144,128]{2,1,0:T(8,128)(2,1)}), bf16[16,144,128]{2,1,0:T(8,128)(2,1)S(1)}, u32[]{:S(2)}, u32[]{:S(2)}) %all-to-all-start) | async-done | bytes 589856 | tf_op jit(solution)/shard_map/all_to_all | solution.py:200
  57.4 0.0 copy-start.1
  57.4 0.0 collective-permute-done.next_ref
  57.4 0.8 copy-done.1
  58.3 0.0 copy-start.2
  58.3 0.8 copy-done.2
  59.1 8.4 %lag_sums.1 = bf16[1024,128]{1,0:T(8,128)(2,1)} custom-call(s32[8]{0:T(128)} %offsets_ref.1, f32[6,128]{1,0:T(8,128)} %reshape.8.weight_ref, bf16[16,144,128]{2,1,0:T(8,128)(2,1)} %copy-done.1, bf16[16,144,128]{2,1,0:T(8,128)(2,1)} %copy-done, bf16[14,144,128]{2,1,0:T(8,128)(2,1)} %copy-done.2, bf16[1152,128]{1,0:T(8,128)(2,1)} %constant.19.clone.gather_ref), custom_call_target="tpu_custom_call" | custom-call | flops 20000000 | bytes 4000000 | tf_op jit(solution)/shard_map/lag_sums/pallas_call | solution.py:144
  67.5 33.5 %all_to_all.15.parts_ref = bf16[128,8,128]{2,1,0:T(8,128)(2,1)} all-to-all(bf16[128,8,128]{2,1,0:T(8,128)(2,1)} %bitcast.1), channel_id=1, replica_groups=mesh['z'=4,'y'=8,'core'=2,'lat'=8] {'lat','y','core'}, dimensions={0} | all-to-all | bytes 524288 | tf_op jit(solution)/shard_map/all_to_all | solution.py:203
  101.0 1.8 %finish.1 = f32[1,24,222]{2,1,0:T(8,128)} custom-call(bf16[128,8,128]{2,1,0:T(8,128)(2,1)} %all_to_all.15.parts_ref), custom_call_target="tpu_custom_call" | custom-call | tf_op jit(solution)/shard_map/finish/pallas_call | solution.py:181
  (1 shorter events, 0.0 us)
Async XLA Ops:
  7.0 28.9 %all-to-all-start.1 = ((bf16[16,144,128]{2,1,0:T(8,128)(2,1)}), bf16[16,144,128]{2,1,0:T(8,128)(2,1)S(1)}, u32[]{:S(2)}, u32[]{:S(2)}) async-start(bf16[16,144,128]{2,1,0:T(8,128)(2,1)} %pack.3), calls=%async_computation.1 | async-start | bytes 1179648 | tf_op jit(solution)/shard_map/all_to_all | solution.py:196
  35.9 3.5 %copy-start = (bf16[16,144,128]{2,1,0:T(8,128)(2,1)}, bf16[16,144,128]{2,1,0:T(8,128)(2,1)S(1)}, u32[]{:S(2)}) copy-start(bf16[16,144,128]{2,1,0:T(8,128)(2,1)S(1)} %all-to-all-done.1.true_ref) | copy-start | bytes 1769476
  35.9 21.5 %all-to-all-start = ((bf16[16,144,128]{2,1,0:T(8,128)(2,1)}), bf16[16,144,128]{2,1,0:T(8,128)(2,1)S(1)}, u32[]{:S(2)}, u32[]{:S(2)}) async-start(bf16[16,144,128]{2,1,0:T(8,128)(2,1)} %pack.2), calls=%async_computation | async-start | bytes 1179648 | tf_op jit(solution)/shard_map/all_to_all | solution.py:200
  39.5 18.0 %collective-permute-start = (bf16[14,144,128]{2,1,0:T(8,128)(2,1)S(1)}, bf16[14,144,128]{2,1,0:T(8,128)(2,1)S(1)}, u32[]{:S(2)}, u32[]{:S(2)}) collective-permute-start(bf16[14,144,128]{2,1,0:T(8,128)(2,1)S(1)} %slice.4), channel_id=1, source_target_pairs={{128,0},{256,128},{384,256},{0,384},{129,1},{257,129},{385,257},{1... | collective-permute-start | bytes 1548296 | tf_op jit(solution)/shard_map/ppermute | solution.py:198
  57.4 0.8 copy-start.1
  58.3 0.8 copy-start.2

commit v2 on v1

v2 whole, which is shorter than its diff:
```python
import jax
import jax.numpy as jnp
from jax import lax
from jax.experimental import pallas as pl
from jax.experimental.pallas import tpu as pltpu
from jax.sharding import Mesh
from jax.sharding import PartitionSpec as P

REG = 0.001
K = 8
ROWS = 48
COLS = 24
CHANNELS = 222
GROUPS = 16
PER = 14
SLOT = 16
SUB = 8
STEPS = ROWS // SUB
BLOCK = GROUPS * COLS
HALO = 14
WINDOW = BLOCK + HALO * COLS
MISSING = 1024.0
LANES = 128


def pack_kernel(field_ref, mean_ref, flags_ref, out_ref, field, mean, low, mid, high, arrived):
    def copies(g):
        rows = pl.ds(g * SUB, SUB)
        return (
            pltpu.make_async_copy(field_ref.at[rows], field.at[rows], arrived.at[0, g]),
            pltpu.make_async_copy(mean_ref.at[rows], mean.at[rows], arrived.at[1, g]),
        )

    for g in range(STEPS):
        for copy in copies(g):
            copy.start()
    lane = lax.broadcasted_iota(jnp.int32, (COLS, LANES), 1)
    valid = flags_ref[...].astype(jnp.float32)
    valid = jnp.concatenate([valid, jnp.zeros((COLS, LANES - ROWS), jnp.float32)], axis=1)
    pad = jnp.zeros((COLS, 2 * LANES - CHANNELS), jnp.float32)

    def group(g, carry):
        for copy in copies(g):
            copy.wait()
        usable = pltpu.roll(valid, LANES - g * SUB, 1)
        for r in range(SUB):
            keep = jnp.broadcast_to(usable[:, r : r + 1], (COLS, LANES)) > 0.5
            row = g * SUB + r
            left = field[row, :, :LANES].astype(jnp.float32) - mean[row, :, :LANES].astype(jnp.float32)
            right = field[row, :, LANES:].astype(jnp.float32) - mean[row, :, LANES:].astype(jnp.float32)
            left = pltpu.roll(jnp.where(keep, left, MISSING), SLOT * r, 1)
            right = pltpu.roll(jnp.where(keep, jnp.concatenate([right, pad], axis=1), MISSING), SLOT * r, 1)
            low[r] = left
            high[r] = right
            mid[r] = jnp.where(((lane - SLOT * r) & (LANES - 1)) >= 9 * PER, left, right)
        for q in range(GROUPS):
            source = low if q < 9 else mid if q == 9 else high
            owner = ((lane - PER * q) & (LANES - 1)) // SLOT
            acc = source[0]
            for r in range(1, SUB):
                acc = jnp.where(owner == r, source[r], acc)
            moved = pltpu.roll(acc, -PER * q % LANES, 1)
            out_ref[q, pl.ds(pl.multiple_of(g * COLS, 8), COLS), :] = moved.astype(jnp.bfloat16)
        return carry

    lax.fori_loop(0, STEPS, group, 0)


def on_chip(mib, flops):
    return dict(
        compiler_params=pltpu.CompilerParams(vmem_limit_bytes=mib * 1024 * 1024),
        cost_estimate=pl.CostEstimate(flops=flops, bytes_accessed=2_000_000, transcendentals=0),
    )


def pack(field, mean, flags):
    vmem, hbm = pl.BlockSpec(memory_space=pltpu.VMEM), pl.BlockSpec(memory_space=pltpu.HBM)
    return pl.pallas_call(
        pack_kernel,
        in_specs=[hbm, hbm, vmem],
        out_specs=vmem,
        out_shape=jax.ShapeDtypeStruct((GROUPS, STEPS * COLS, LANES), jnp.bfloat16),
        scratch_shapes=[pltpu.VMEM((ROWS, COLS, CHANNELS), jnp.bfloat16)] * 2
        + [pltpu.VMEM((SUB, COLS, LANES), jnp.float32)] * 3
        + [pltpu.SemaphoreType.DMA((2, STEPS))],
        name="pack",
        **on_chip(62, 4_000_000),
    )(field, mean, flags)


def totals_at(k, t):
    return pl.ds(pl.multiple_of((k * GROUPS + t) * 8, 8), 8)


def halves_of(value):
    first = value.astype(jnp.bfloat16)
    return first, (value - first.astype(jnp.float32)).astype(jnp.bfloat16)


def gather_matrix(n):
    row = lax.broadcasted_iota(jnp.int32, (3 * LANES, LANES), 0)
    lane = lax.broadcasted_iota(jnp.int32, (3 * LANES, LANES), 1)
    channel = row & (SLOT - 1)
    target = channel + PER * (3 * n + row // LANES)
    return jnp.where((channel < PER) & (lane == target), 1.0, 0.0).astype(jnp.bfloat16)


def dot(a, b):
    return jnp.dot(a, b, preferred_element_type=jnp.float32)


def true_kernel(offsets_ref, weight_ref, true_ref, next_ref, out_ref, usable, square, total):
    def unpack(source, first):
        def run(p, carry):
            for g in range(STEPS):
                at = pl.ds(pl.multiple_of(g * WINDOW + first + p * COLS, 8), COLS)
                value = source[p, g * COLS : (g + 1) * COLS, :].astype(jnp.float32)
                keep = value < MISSING / 2
                square[at, :] = jnp.where(keep, value * value, 0.0)
                if first == 0:
                    usable[at, :] = jnp.where(keep, weight_ref[g : g + 1, :], 0.0)
            return carry

        return run

    lax.fori_loop(0, GROUPS, unpack(true_ref, 0), 0)
    lax.fori_loop(0, HALO, unpack(next_ref, BLOCK), 0)
    lag = [offsets_ref[k] for k in range(K)]

    def tile(t, carry):
        for part in range(COLS // 8):
            start = t * COLS + part * 8
            acc = [jnp.zeros((8, LANES), jnp.float32)] * K
            for g in range(STEPS):
                d = usable[pl.ds(pl.multiple_of(g * WINDOW + start, 8), 8), :]
                for k in range(K):
                    acc[k] = acc[k] + d * square[pl.ds(g * WINDOW + start + lag[k], 8), :]
            for k in range(K):
                total[totals_at(k, t), part * LANES : part * LANES + LANES] = acc[k]
        return carry

    lax.fori_loop(0, GROUPS, tile, 0)
    first, second = halves_of(total[...])
    gather = gather_matrix(2)
    out_ref[...] = (dot(first, gather) + dot(second, gather)).astype(jnp.bfloat16)


def fore_kernel(offsets_ref, weight_ref, fore_ref, true_ref, next_ref, true_sums_ref, out_ref, cross, spread, shifted, usable, total):
    def unpack(source, first):
        def run(p, carry):
            for g in range(STEPS):
                rows = slice(g * COLS, (g + 1) * COLS)
                at = pl.ds(pl.multiple_of(g * WINDOW + first + p * COLS, 8), COLS)
                value = source[p, rows, :].astype(jnp.float32)
                keep = value < MISSING / 2
                shifted[at, :] = jnp.where(keep, value, 0.0)
                usable[at, :] = jnp.where(keep, 1.0, 0.0)
                if first == 0:
                    at = pl.ds(pl.multiple_of(g * BLOCK + p * COLS, 8), COLS)
                    value = jnp.where(keep, fore_ref[p, rows, :].astype(jnp.float32), 0.0)
                    scaled = value * weight_ref[g : g + 1, :]
                    cross[at, :] = scaled
                    spread[at, :] = scaled * value
            return carry

        return run

    lax.fori_loop(0, GROUPS, unpack(true_ref, 0), 0)
    lax.fori_loop(0, HALO, unpack(next_ref, BLOCK), 0)
    lag = [offsets_ref[k] for k in range(K)]

    def tile(t, carry):
        for part in range(COLS // 8):
            start = t * COLS + part * 8
            acc = [[jnp.zeros((8, LANES), jnp.float32)] * 2 for _ in range(K)]
            for g in range(STEPS):
                at = pl.ds(pl.multiple_of(g * BLOCK + start, 8), 8)
                a, c = cross[at, :], spread[at, :]
                for k in range(K):
                    there = pl.ds(g * WINDOW + start + lag[k], 8)
                    acc[k] = [acc[k][0] + a * shifted[there, :], acc[k][1] + c * usable[there, :]]
            for k in range(K):
                for n in range(2):
                    column = (n * 3 + part) * LANES
                    total[totals_at(k, t), column : column + LANES] = acc[k][n]
        return carry

    lax.fori_loop(0, GROUPS, tile, 0)
    first, second = halves_of(total[:, : 3 * LANES])
    gather = gather_matrix(0)
    out = dot(first, gather) + dot(second, gather)
    out += dot(total[:, 3 * LANES :].astype(jnp.bfloat16), gather_matrix(1))
    out_ref[...] = (true_sums_ref[...].astype(jnp.float32) + out).astype(jnp.bfloat16)


def window_call(kernel, inputs, scratch, name, flops):
    vmem = pl.BlockSpec(memory_space=pltpu.VMEM)
    return pl.pallas_call(
        kernel,
        in_specs=[pl.BlockSpec(memory_space=pltpu.SMEM)] + [vmem] * (len(inputs) - 1),
        out_specs=vmem,
        out_shape=jax.ShapeDtypeStruct((K * GROUPS * 8, LANES), jnp.bfloat16),
        scratch_shapes=[pltpu.VMEM((rows, lanes), jnp.float32) for rows, lanes in scratch],
        name=name,
        **on_chip(28, flops),
    )(*inputs)


def finish_kernel(parts_ref, out_ref):
    lane = lax.broadcasted_iota(jnp.int32, (8, LANES), 1)
    halves = [[jnp.zeros((8, LANES), jnp.float32)] * 2 for _ in range(3)]
    for q in range(GROUPS):
        total = parts_ref[q].astype(jnp.float32)
        for device in range(1, K):
            total = total + parts_ref[device * GROUPS + q].astype(jnp.float32)
        fore = pltpu.roll(total, LANES - 3 * PER, 1)
        true = pltpu.roll(total, LANES - 6 * PER, 1)
        value = total / jnp.sqrt((fore + REG) * (true + REG))
        low, high = PER * q, PER * q + PER
        for part in range(3):
            moved = pltpu.roll(value, (PER * q - PER * part) % LANES, 1)
            for half in range(2):
                at = lane + half * LANES
                if low < (half + 1) * LANES and high > half * LANES:
                    halves[part][half] = jnp.where((at >= low) & (at < high), moved, halves[part][half])
    for part in range(3):
        out_ref[0, part * 8 : part * 8 + 8, :LANES] = halves[part][0]
        out_ref[0, part * 8 : part * 8 + 8, LANES:] = halves[part][1][:, : CHANNELS - LANES]


def finish(parts):
    vmem = pl.BlockSpec(memory_space=pltpu.VMEM)
    return pl.pallas_call(
        finish_kernel,
        in_specs=[vmem],
        out_specs=vmem,
        out_shape=jax.ShapeDtypeStruct((1, COLS, CHANNELS), jnp.float32),
        name="finish",
        **on_chip(4, 1_000_000),
    )(parts)


def local(prediction, observed_state, mean_state, usable_point_flags, eastward_offsets):
    row = lax.axis_index("lat") * ROWS + jnp.arange(ROWS, dtype=jnp.int32)
    weight = jnp.cos(jnp.pi * ((row.astype(jnp.float32) + 0.5) / (ROWS * lax.axis_size("lat")) - 0.5))
    weight = jnp.repeat(weight.reshape(STEPS, SUB), SLOT, axis=1)
    flags = usable_point_flags.T
    around = ("y", "core")
    true = pack(observed_state, mean_state, flags)
    true = lax.all_to_all(true, around, 0, 0, tiled=True)
    count = lax.axis_size("z")
    following = lax.ppermute(true[:HALO], "z", [((i + 1) % count, i) for i in range(count)])
    fore = pack(prediction, mean_state, flags)
    fore = lax.all_to_all(fore, around, 0, 0, tiled=True)
    own, window, totals = (STEPS * BLOCK, LANES), (STEPS * WINDOW, LANES), K * GROUPS * 8
    true_sums = window_call(
        true_kernel,
        (eastward_offsets, weight, true, following),
        (window, window, (totals, 3 * LANES)),
        "true_side",
        8_000_000,
    )
    sums = window_call(
        fore_kernel,
        (eastward_offsets, weight, fore, true, following, true_sums),
        (own, own, window, window, (totals, 6 * LANES)),
        "fore_side",
        12_000_000,
    )
    parts = sums.reshape(K * GROUPS, 8, LANES)
    parts = lax.all_to_all(parts, ("lat",) + around, 0, 0, tiled=True)
    return finish(parts)


def solution(mesh):
    split = Mesh(mesh.devices.reshape(4, 8, 2, 8), ("z", "y", "core", "lat"))
    lon = ("z", "y", "core")
    placed = (P("lat", lon, None), P("lat", lon, None), P("lat", lon, None), P("lat", lon), P())
    return jax.shard_map(local, mesh=split, in_specs=placed, out_specs=P("lat", lon, None), check_vma=False)
```

time: 104 us -> 97.3 us (0.936)
  Pallas kernels: 21.3 us -> 17 us
  local copies, waits for them, and re-layouts: 3.83 us -> 0.19 us
  blocking collectives: 33.5 us -> 34.8 us
    all_to_all x1, waiting for transfers between devices: 11.3 us -> 0.01 us  [local(): fore = lax.all_to_all(fore, around, 0, 0, tiled=True)]
    ppermute x1, waiting for transfers between devices: 0.01 us -> 11.2 us  [local(): lax.ppermute(true[:HALO], 'z', [((i + 1) % count, i) for i in range(count)])]
    pallas_call x3 -> x4, Pallas kernels: 19.6 us -> 16.2 us  [the longest x2 9.47 us: pack(): pl.pallas_call(pack_kernel, in_specs=[hbm, hbm, vmem], out_specs=vmem, ou...]
    unnamed x7 -> x2, local copies, waits for them, and re-layouts: 3.05 us -> 0.01 us
    all_to_all x1, blocking collectives: 33.5 us -> 34.8 us  [local(): parts = lax.all_to_all(parts, ('lat',) + around, 0, 0, tiled=True)]
  transfers between devices with their start and end apart: 3 -> 3, of which waited for: 2 -> 2; matrix products, arithmetic and copies ran while one was open for 1% -> 0% of each run, Pallas kernels for 5% -> 8%
where the time goes in v2:
time: 97.3 us; the launch traced here: 96.8 us
  blocking collectives  34.8 us (36%)
  waiting for transfers between devices  25.2 us (26%)
  starting transfers between devices  19.5 us (20%)
  Pallas kernels  17 us (17%)
    all_to_all x1, blocking collectives, local(): parts = lax.all_to_all(parts, ('lat',) + around, 0, 0, tiled=True)  34.8 us
    all_to_all x1, waiting for transfers between devices, local(): true = lax.all_to_all(true, around, 0, 0, tiled=True)  14 us
    ppermute x1, waiting for transfers between devices, local(): lax.ppermute(true[:HALO], 'z', [((i + 1) % count, i) for i in range(count)])  11.2 us
    all_to_all x1, starting transfers between devices, local(): true = lax.all_to_all(true, around, 0, 0, tiled=True)  10.2 us
    pallas_call x2, Pallas kernels, pack(): pl.pallas_call(pack_kernel, in_specs=[hbm, hbm, vmem], out_specs=vmem, ou...  9.47 us
    pallas_call x2, Pallas kernels, window_call(): pl.pallas_call(kernel, in_specs=[pl.BlockSpec(memory_space=pltpu.SMEM)] +...  6.7 us
    ppermute x1, starting transfers between devices, local(): lax.ppermute(true[:HALO], 'z', [((i + 1) % count, i) for i in range(count)])  5.84 us
    all_to_all x1, starting transfers between devices, local(): fore = lax.all_to_all(fore, around, 0, 0, tiled=True)  3.48 us
  transfers between devices with their start and end apart: 3, of which 2 were waited for; matrix products, arithmetic and copies ran while one was open for 0% of the time, Pallas kernels for 8%

profile of v2, /device:TPU:1, one launch (start us, length us, event | category | flops | bytes accessed | tf_op | source)
XLA Modules:
  0.0 96.8 jit_solution(15533219612028360639)
XLA Ops:
  0.0 4.7 %pack.3 = bf16[16,144,128]{2,1,0:T(8,128)(2,1)} custom-call(bf16[48,24,222]{2,1,0:T(8,128)(2,1)} %field_ref.3, bf16[48,24,222]{2,1,0:T(8,128)(2,1)} %mean_ref.3, s32[24,48]{1,0:T(8,128)} %bitcast.3), custom_call_target="tpu_custom_call" | custom-call | flops 4000000 | bytes 2000000 | tf_op jit(solution)/shard_map/pack/pallas_call | solution.py:78
  4.7 10.2 %all-to-all-start.1 = ((bf16[16,144,128]{2,1,0:T(8,128)(2,1)}), bf16[16,144,128]{2,1,0:T(8,128)(2,1)S(1)}, u32[]{:S(2)}, u32[]{:S(2)}) async-start(bf16[16,144,128]{2,1,0:T(8,128)(2,1)} %pack.3), calls=%async_computation.1 | async-start | bytes 1179648 | tf_op jit(solution)/shard_map/all_to_all | solution.py:250
  15.0 4.7 %pack.2 = bf16[16,144,128]{2,1,0:T(8,128)(2,1)} custom-call(bf16[48,24,222]{2,1,0:T(8,128)(2,1)} %field_ref.2, bf16[48,24,222]{2,1,0:T(8,128)(2,1)} %mean_ref.3, s32[24,48]{1,0:T(8,128)} %bitcast.4), custom_call_target="tpu_custom_call" | custom-call | flops 4000000 | bytes 2000000 | tf_op jit(solution)/shard_map/pack/pallas_call | solution.py:78
  19.7 14.0 %all-to-all-done.1.true_ref = bf16[16,144,128]{2,1,0:T(8,128)(2,1)S(1)} async-done(((bf16[16,144,128]{2,1,0:T(8,128)(2,1)}), bf16[16,144,128]{2,1,0:T(8,128)(2,1)S(1)}, u32[]{:S(2)}, u32[]{:S(2)}) %all-to-all-start.1) | async-done | bytes 589856 | tf_op jit(solution)/shard_map/all_to_all | solution.py:250
  33.7 3.5 %all-to-all-start = ((bf16[16,144,128]{2,1,0:T(8,128)(2,1)}), bf16[16,144,128]{2,1,0:T(8,128)(2,1)S(1)}, u32[]{:S(2)}, u32[]{:S(2)}) async-start(bf16[16,144,128]{2,1,0:T(8,128)(2,1)} %pack.2), calls=%async_computation | async-start | bytes 1179648 | tf_op jit(solution)/shard_map/all_to_all | solution.py:254
  37.2 5.8 %collective-permute-start = (bf16[14,144,128]{2,1,0:T(8,128)(2,1)S(1)}, bf16[14,144,128]{2,1,0:T(8,128)(2,1)S(1)}, u32[]{:S(2)}, u32[]{:S(2)}) collective-permute-start(bf16[14,144,128]{2,1,0:T(8,128)(2,1)S(1)} %slice.4), channel_id=1, source_target_pairs={{128,0},{256,128},{384,256},{0,384},{129,1},{257,129},{385,257},{1... | collective-permute-start | bytes 1548296 | tf_op jit(solution)/shard_map/ppermute | solution.py:252
  43.1 0.1 multiply_cosine_fusion
  43.1 0.1 broadcast_in_dim.3
  43.2 0.0 copy-start
  43.2 0.1 reshape.8.weight_ref
  43.3 11.2 %collective-permute-done.next_ref = bf16[14,144,128]{2,1,0:T(8,128)(2,1)S(1)} collective-permute-done((bf16[14,144,128]{2,1,0:T(8,128)(2,1)S(1)}, bf16[14,144,128]{2,1,0:T(8,128)(2,1)S(1)}, u32[]{:S(2)}, u32[]{:S(2)}) %collective-permute-start) | collective-permute-done | bytes 516128 | tf_op jit(solution)/shard_map/ppermute | solution.py:252
  54.5 0.0 copy-done
  54.5 2.6 %true_side.1.true_sums_ref = bf16[1024,128]{1,0:T(8,128)(2,1)S(1)} custom-call(s32[8]{0:T(128)S(1)} %copy-done, f32[6,128]{1,0:T(8,128)S(1)} %reshape.8.weight_ref, bf16[16,144,128]{2,1,0:T(8,128)(2,1)S(1)} %all-to-all-done.1.true_ref, bf16[14,144,128]{2,1,0:T(8,128)(2,1)S(1)} %collective-permute-done.next_ref), custom_call_target="tpu_custom_call" | custom-call | flops 8000000 | bytes 2000000 | tf_op jit(solution)/shard_map/true_side/pallas_call | solution.py:198
  57.1 0.0 all-to-all-done.fore_ref
  57.1 4.1 %fore_side.1 = bf16[1024,128]{1,0:T(8,128)(2,1)S(1)} custom-call(s32[8]{0:T(128)S(1)} %copy-done, f32[6,128]{1,0:T(8,128)S(1)} %reshape.8.weight_ref, bf16[16,144,128]{2,1,0:T(8,128)(2,1)S(1)} %all-to-all-done.fore_ref, bf16[16,144,128]{2,1,0:T(8,128)(2,1)S(1)} %all-to-all-done.1.true_ref, bf16[14,144,128]{2,1,0:T(8,128)(2,1)S(1)} %collective-permute-done.next_ref, ...), custom_call_target="tpu_custom_call" | custom-call | flops 12000000 | bytes 2000000 | tf_op jit(solution)/shard_map/fore_side/pallas_call | solution.py:198
  61.2 34.8 %all_to_all.15.parts_ref = bf16[128,8,128]{2,1,0:T(8,128)(2,1)S(1)} all-to-all(bf16[128,8,128]{2,1,0:T(8,128)(2,1)S(1)} %bitcast.2), channel_id=1, replica_groups=mesh['z'=4,'y'=8,'core'=2,'lat'=8] {'lat','y','core'}, dimensions={0} | all-to-all | bytes 524288 | tf_op jit(solution)/shard_map/all_to_all | solution.py:271
  96.0 0.8 finish.1
  (1 shorter events, 0.0 us)
Async XLA Ops:
  4.7 28.9 %all-to-all-start.1 = ((bf16[16,144,128]{2,1,0:T(8,128)(2,1)}), bf16[16,144,128]{2,1,0:T(8,128)(2,1)S(1)}, u32[]{:S(2)}, u32[]{:S(2)}) async-start(bf16[16,144,128]{2,1,0:T(8,128)(2,1)} %pack.3), calls=%async_computation.1 | async-start | bytes 1179648 | tf_op jit(solution)/shard_map/all_to_all | solution.py:250
  33.7 23.4 %all-to-all-start = ((bf16[16,144,128]{2,1,0:T(8,128)(2,1)}), bf16[16,144,128]{2,1,0:T(8,128)(2,1)S(1)}, u32[]{:S(2)}, u32[]{:S(2)}) async-start(bf16[16,144,128]{2,1,0:T(8,128)(2,1)} %pack.2), calls=%async_computation | async-start | bytes 1179648 | tf_op jit(solution)/shard_map/all_to_all | solution.py:254
  37.2 17.3 %collective-permute-start = (bf16[14,144,128]{2,1,0:T(8,128)(2,1)S(1)}, bf16[14,144,128]{2,1,0:T(8,128)(2,1)S(1)}, u32[]{:S(2)}, u32[]{:S(2)}) collective-permute-start(bf16[14,144,128]{2,1,0:T(8,128)(2,1)S(1)} %slice.4), channel_id=1, source_target_pairs={{128,0},{256,128},{384,256},{0,384},{129,1},{257,129},{385,257},{1... | collective-permute-start | bytes 1548296 | tf_op jit(solution)/shard_map/ppermute | solution.py:252
  43.2 11.3 %copy-start = (s32[8]{0:T(128)S(1)}, s32[8]{0:T(128)}, u32[]{:S(2)}) copy-start(s32[8]{0:T(128)} %offsets_ref.3) | copy-start | bytes 100
